TPU v7x, 32 devices: a 4x4x1 block of a 4x4x8 slice. The times are simulated.
32 devices in a mesh: batch: 1 (over z), col: 4 (over y), row: 8 (over x, core).
Axes of the slice: x: 4, y: 4, z: 1, core: 2. Of those that a mesh axis runs over, the one named last changes fastest.
The devices are a block of a 4x4x8 slice.
Arguments:
- z_one: bfloat16 [1024, 1024, 64], P(('batch', 'row'), 'col')
- z_two: bfloat16 [1024, 1024, 64], P(('batch', 'row'), 'col')
- mask_one: int32 [1024, 1024], P(('batch', 'row'), 'col')
- mask_two: int32 [1024, 1024], P(('batch', 'row'), 'col')
- ln_in_scale: bfloat16 [64], replicated
- w_a: bfloat16 [64, 64], replicated
- w_a_gate: bfloat16 [64, 64], replicated
- w_b: bfloat16 [64, 64], replicated
- w_b_gate: bfloat16 [64, 64], replicated
- w_gate: bfloat16 [64, 64], replicated
- w_out: bfloat16 [64, 64], replicated
- ln_out_scale: bfloat16 [64], replicated
Outputs:
- output 1: bfloat16 [1024, 1024, 64], P(('batch', 'row'), 'col')
- output 2: bfloat16 [1024, 1024, 64], P(('batch', 'row'), 'col')
All inputs are finite; a program needn't handle non-finite values.
Results may differ from a plain program's by a relative error of at most 0.001.
Values are sent between devices in bfloat16 or wider.
A program may use at most 768 MiB of HBM per device.

v0:
```python
import math
import jax
import jax.numpy as jnp
from jax import lax
from jax.sharding import PartitionSpec as P


def layer_norm(values, scale):
    row_mean = jnp.mean(values, axis=-1, keepdims=True)
    centered = values - row_mean
    variance = jnp.mean(centered * centered, axis=-1, keepdims=True)
    return centered * lax.rsqrt(variance + 1e-5) * scale.astype(jnp.float32)


def tile_update(pair_tile, mask_tile, ln_in_scale, weights, transpose_perm, col_count, ratio):
    w_a, w_a_gate, w_b, w_b_gate, w_gate, w_out, ln_out_scale = weights
    rows_loc, cols_loc, pair_ch = pair_tile.shape
    hidden = w_out.shape[0]
    normed = layer_norm(pair_tile.astype(jnp.float32), ln_in_scale).astype(jnp.bfloat16)

    def project(source, weight):
        return jnp.einsum('ijd,de->ije', source, weight, preferred_element_type=jnp.float32)

    mask_val = mask_tile.astype(jnp.float32)[:, :, None]
    left = (mask_val * jax.nn.sigmoid(project(normed, w_a_gate)) * project(normed, w_a)).astype(jnp.bfloat16)
    right = (mask_val * jax.nn.sigmoid(project(normed, w_b_gate)) * project(normed, w_b)).astype(jnp.bfloat16)
    left_rows = lax.all_gather(left, 'col', axis=1)
    right_moved = lax.ppermute(right, ('col', 'row'), transpose_perm)
    right_rows = lax.all_gather(right_moved, 'row', axis=0).reshape(col_count, ratio, rows_loc, cols_loc, hidden)
    block_rows = math.gcd(rows_loc, 32)
    block_count = rows_loc // block_rows

    def finish(block):
        left_blk, pair_blk, normed_blk = block
        contracted = jnp.einsum('itkc,tujkc->iujc', left_blk, right_rows, preferred_element_type=jnp.float32)
        contracted = contracted.reshape(block_rows, cols_loc, hidden)
        normed_out = layer_norm(contracted, ln_out_scale).astype(jnp.bfloat16)
        update = jnp.einsum('ijc,cd->ijd', normed_out, w_out, preferred_element_type=jnp.float32)
        gate = jax.nn.sigmoid(project(normed_blk, w_gate))
        return (pair_blk.astype(jnp.float32) + gate * update).astype(jnp.bfloat16)

    out_blocks = lax.map(finish, (
        left_rows.reshape(block_count, block_rows, col_count, cols_loc, hidden),
        pair_tile.reshape(block_count, block_rows, cols_loc, pair_ch),
        normed.reshape(block_count, block_rows, cols_loc, pair_ch),
    ))
    return out_blocks.reshape(rows_loc, cols_loc, pair_ch)


def solution(mesh):
    row_count = mesh.shape['row']
    col_count = mesh.shape['col']
    ratio = row_count // col_count
    transpose_perm = [
        (src_col * row_count + src_row, (src_row // ratio) * row_count + src_col * ratio + src_row % ratio)
        for src_row in range(row_count) for src_col in range(col_count)
    ]
    pair_spec = P(('batch', 'row'), 'col', None)
    mask_spec = P(('batch', 'row'), 'col')
    replicated = P()

    def device_fn(z_one, z_two, mask_one, mask_two, ln_in_scale, w_a, w_a_gate, w_b, w_b_gate, w_gate, w_out, ln_out_scale):
        weights = (w_a, w_a_gate, w_b, w_b_gate, w_gate, w_out, ln_out_scale)
        out_one = tile_update(z_one, mask_one, ln_in_scale, weights, transpose_perm, col_count, ratio)
        out_two = tile_update(z_two, mask_two, ln_in_scale, weights, transpose_perm, col_count, ratio)
        return out_one, out_two

    return jax.shard_map(
        device_fn,
        mesh=mesh,
        in_specs=(pair_spec, pair_spec, mask_spec, mask_spec, replicated, replicated, replicated, replicated, replicated, replicated, replicated, replicated),
        out_specs=(pair_spec, pair_spec),
        check_vma=False,
    )
```

profile of v0, /device:TPU:97, one launch (start us, length us, event | category | flops | bytes accessed | tf_op | source)
XLA Modules:
  0.0 1178.8 jit_solution(11588942637020274189)
XLA Ops:
  7.3 3.7 convert_reduce_fusion
  16.7 5.7 fusion.36
  24.4 4.4 multiply_convert_fusion.5
  29.8 3.6 fusion.50
  33.4 4.5 multiply_convert_fusion.7
  38.6 3.6 fusion.42
  42.3 3.1 multiply_convert_fusion.4
  48.2 3.6 fusion.44
  51.8 3.1 multiply_convert_fusion.6
  55.0 2.8 collective-permute-start
  58.1 481.6 %all-gather.13.cloned.1.call-done = bf16[128,1024,64]{1,2,0:T(8,128)(2,1)} async-done(((bf16[128,256,64]{1,2,0:T(8,128)(2,1)}), bf16[128,1024,64]{1,2,0:T(8,128)(2,1)}) %all-gather.13.cloned.1.call-update) | async-done | bytes 16777232 | tf_op jit(solution)/shard_map/all_gather | solution.py:27
  539.7 27.9 %reshape.142 = bf16[4,32,4,256,64]{3,2,4,1,0:T(4,128)(2,1)} reshape(bf16[128,1024,64]{1,2,0:T(8,128)(2,1)} %all-gather.13.cloned.1.call-done) | data formatting | bytes 33554432 | tf_op jit(solution)/shard_map/reshape | solution.py:43
  567.6 132.0 %all-gather.9.cloned.1.call-done = bf16[128,1024,64]{1,2,0:T(8,128)(2,1)} async-done(((bf16[128,256,64]{1,2,0:T(8,128)(2,1)}), bf16[128,1024,64]{1,2,0:T(8,128)(2,1)}) %all-gather.9.cloned.1.call-update) | async-done | bytes 16777232 | tf_op jit(solution)/shard_map/all_gather | solution.py:27
  699.6 27.9 %reshape.137 = bf16[4,32,4,256,64]{3,2,4,1,0:T(4,128)(2,1)} reshape(bf16[128,1024,64]{1,2,0:T(8,128)(2,1)} %all-gather.9.cloned.1.call-done) | data formatting | bytes 33554432 | tf_op jit(solution)/shard_map/reshape | solution.py:43
  727.4 130.0 %all-gather.15.cloned.1.call-done = bf16[1024,256,64]{1,2,0:T(8,128)(2,1)} async-done(((bf16[128,256,64]{1,2,0:T(8,128)(2,1)}), bf16[1024,256,64]{1,2,0:T(8,128)(2,1)}) %all-gather.15.cloned.1.call-update) | async-done | bytes 33554448 | tf_op jit(solution)/shard_map/all_gather | solution.py:29
  857.5 23.3 %copy.70 = bf16[4,2,128,256,64]{3,2,0,1,4:T(8,128)(2,1)} copy(bf16[4,2,128,256,64]{3,4,2,1,0:T(8,128)(2,1)} %bitcast.175) | data formatting | bytes 67108864 | tf_op jit(solution)/shard_map/while | solution.py:42
  883.4 130.6 %while.21 = (s32[]{:T(128)}, bf16[4,32,256,64]{2,3,1,0:T(8,128)(2,1)}, bf16[4,32,256,64]{2,3,1,0:T(8,128)(2,1)}, bf16[4,32,256,64]{2,3,1,0:T(8,128)(2,1)}, bf16[...) while((s32[]{:T(128)}, ...), condition=%wide.region_11.12_spmd, body=%wide.region_8.11_spmd.sunk | while | flops 1215832064 | bytes 68568808 | solution.py:42
  883.4 6.6 constant_dynamic-slice_fusion.5
  890.0 15.9 %fusion.93 = (f32[32,2,128]{2,0,1:T(8,128)S(1)}, f32[32,2,128,64]{2,0,1,3:T(8,128)S(1)}) fusion(bf16[4,2,128,256,64]{3,2,0,1,4:T(8,128)(2,1)} %get-tuple-element.394, bf16[1,32,4,256,64]{3,2,4,1,0:T(4,128)(2,1)} %constant_dynamic-slice_fusion.5), kind=kOutput, calls=%fused_computation.83.clone.1 | convolution fusion | flops 1074257920 | bytes 39878656 | tf_op jit(solution)/shard_map/while/body/eval_jaxpr/itkc,tujkc->iujc/dot_general | solution.py:35
  907.9 2.7 reshape.174
  912.2 3.8 fusion.95
  916.0 6.6 constant_dynamic-slice_fusion.5
  922.6 15.9 %fusion.93 = (f32[32,2,128]{2,0,1:T(8,128)S(1)}, f32[32,2,128,64]{2,0,1,3:T(8,128)S(1)}) fusion(bf16[4,2,128,256,64]{3,2,0,1,4:T(8,128)(2,1)} %get-tuple-element.394, bf16[1,32,4,256,64]{3,2,4,1,0:T(4,128)(2,1)} %constant_dynamic-slice_fusion.5), kind=kOutput, calls=%fused_computation.83.clone.1 | convolution fusion | flops 1074257920 | bytes 39878656 | tf_op jit(solution)/shard_map/while/body/eval_jaxpr/itkc,tujkc->iujc/dot_general | solution.py:35
  944.9 3.8 fusion.95
  948.7 6.6 constant_dynamic-slice_fusion.5
  955.3 15.9 %fusion.93 = (f32[32,2,128]{2,0,1:T(8,128)S(1)}, f32[32,2,128,64]{2,0,1,3:T(8,128)S(1)}) fusion(bf16[4,2,128,256,64]{3,2,0,1,4:T(8,128)(2,1)} %get-tuple-element.394, bf16[1,32,4,256,64]{3,2,4,1,0:T(4,128)(2,1)} %constant_dynamic-slice_fusion.5), kind=kOutput, calls=%fused_computation.83.clone.1 | convolution fusion | flops 1074257920 | bytes 39878656 | tf_op jit(solution)/shard_map/while/body/eval_jaxpr/itkc,tujkc->iujc/dot_general | solution.py:35
  977.5 3.8 fusion.95
  981.3 6.6 constant_dynamic-slice_fusion.5
  988.0 15.9 %fusion.93 = (f32[32,2,128]{2,0,1:T(8,128)S(1)}, f32[32,2,128,64]{2,0,1,3:T(8,128)S(1)}) fusion(bf16[4,2,128,256,64]{3,2,0,1,4:T(8,128)(2,1)} %get-tuple-element.394, bf16[1,32,4,256,64]{3,2,4,1,0:T(4,128)(2,1)} %constant_dynamic-slice_fusion.5), kind=kOutput, calls=%fused_computation.83.clone.1 | convolution fusion | flops 1074257920 | bytes 39878656 | tf_op jit(solution)/shard_map/while/body/eval_jaxpr/itkc,tujkc->iujc/dot_general | solution.py:35
  1010.2 3.8 fusion.95
  1014.1 23.3 %copy.62 = bf16[4,2,128,256,64]{3,2,0,1,4:T(8,128)(2,1)} copy(bf16[4,2,128,256,64]{3,4,2,1,0:T(8,128)(2,1)} %bitcast.174) | data formatting | bytes 67108864 | tf_op jit(solution)/shard_map/while | solution.py:42
  1040.0 131.1 %while.20 = (s32[]{:T(128)}, bf16[4,32,256,64]{2,3,1,0:T(8,128)(2,1)}, bf16[4,32,256,64]{2,3,1,0:T(8,128)(2,1)}, bf16[4,32,256,64]{2,3,1,0:T(8,128)(2,1)}, bf16[...) while((s32[]{:T(128)}, ...), condition=%wide.region_5.6_spmd, body=%wide.region_2.5_spmd.sunk | while | flops 1215832064 | bytes 68568808 | solution.py:42
  1040.2 6.7 constant_dynamic-slice_fusion.4
  1046.9 15.9 %fusion.85 = (f32[32,2,128]{2,0,1:T(8,128)S(1)}, f32[32,2,128,64]{2,0,1,3:T(8,128)S(1)}) fusion(bf16[4,2,128,256,64]{3,2,0,1,4:T(8,128)(2,1)} %get-tuple-element.364, bf16[1,32,4,256,64]{3,2,4,1,0:T(4,128)(2,1)} %constant_dynamic-slice_fusion.4), kind=kOutput, calls=%fused_computation.82.clone.1 | convolution fusion | flops 1074257920 | bytes 39878656 | tf_op jit(solution)/shard_map/while/body/eval_jaxpr/itkc,tujkc->iujc/dot_general | solution.py:35
  1064.8 2.7 reshape.173
  1069.1 3.8 fusion.87
  1072.9 6.7 constant_dynamic-slice_fusion.4
  1079.6 15.9 %fusion.85 = (f32[32,2,128]{2,0,1:T(8,128)S(1)}, f32[32,2,128,64]{2,0,1,3:T(8,128)S(1)}) fusion(bf16[4,2,128,256,64]{3,2,0,1,4:T(8,128)(2,1)} %get-tuple-element.364, bf16[1,32,4,256,64]{3,2,4,1,0:T(4,128)(2,1)} %constant_dynamic-slice_fusion.4), kind=kOutput, calls=%fused_computation.82.clone.1 | convolution fusion | flops 1074257920 | bytes 39878656 | tf_op jit(solution)/shard_map/while/body/eval_jaxpr/itkc,tujkc->iujc/dot_general | solution.py:35
  1097.5 2.7 reshape.173
  1101.9 3.8 fusion.87
  1105.7 6.7 constant_dynamic-slice_fusion.4
  1112.3 15.9 %fusion.85 = (f32[32,2,128]{2,0,1:T(8,128)S(1)}, f32[32,2,128,64]{2,0,1,3:T(8,128)S(1)}) fusion(bf16[4,2,128,256,64]{3,2,0,1,4:T(8,128)(2,1)} %get-tuple-element.364, bf16[1,32,4,256,64]{3,2,4,1,0:T(4,128)(2,1)} %constant_dynamic-slice_fusion.4), kind=kOutput, calls=%fused_computation.82.clone.1 | convolution fusion | flops 1074257920 | bytes 39878656 | tf_op jit(solution)/shard_map/while/body/eval_jaxpr/itkc,tujkc->iujc/dot_general | solution.py:35
  1130.2 2.7 reshape.173
  1134.6 3.8 fusion.87
  1138.4 6.7 constant_dynamic-slice_fusion.4
  1145.1 15.9 %fusion.85 = (f32[32,2,128]{2,0,1:T(8,128)S(1)}, f32[32,2,128,64]{2,0,1,3:T(8,128)S(1)}) fusion(bf16[4,2,128,256,64]{3,2,0,1,4:T(8,128)(2,1)} %get-tuple-element.364, bf16[1,32,4,256,64]{3,2,4,1,0:T(4,128)(2,1)} %constant_dynamic-slice_fusion.4), kind=kOutput, calls=%fused_computation.82.clone.1 | convolution fusion | flops 1074257920 | bytes 39878656 | tf_op jit(solution)/shard_map/while/body/eval_jaxpr/itkc,tujkc->iujc/dot_general | solution.py:35
  1162.9 2.7 reshape.173
  1167.3 3.8 fusion.87
  (111 shorter events, 54.9 us)
Async XLA Ops:
  7.2 15.2 %copy-start = (bf16[64,64]{1,0:T(8,128)(2,1)S(1)}, bf16[64,64]{1,0:T(8,128)(2,1)}, u32[]{:S(2)}) copy-start(bf16[64,64]{1,0:T(8,128)(2,1)} %param.22) | copy-start | bytes 24580
  7.2 532.5 %all-gather.13.cloned.1.call-start = ((), (), s32[]{:S(2)}) async-start(), calls=%async_computation.2 | async-start | bytes 20971520 | tf_op jit(solution)/shard_map/all_gather | solution.py:27
  7.3 3.7 copy-start.6
  7.3 5.8 copy-start.7
  13.1 3.5 copy-start.15
  13.1 3.5 copy-start.8
  22.4 2.0 copy-start.4
  22.4 2.0 copy-start.13
  28.9 0.9 copy-start.9
  28.9 670.7 %all-gather.9.cloned.1.call-start = ((), (), s32[]{:S(2)}) async-start(), calls=%async_computation | async-start | bytes 20971520 | tf_op jit(solution)/shard_map/all_gather | solution.py:27
  29.8 3.7 copy-start.2
  37.9 0.7 copy-start.10
  38.0 4.3 copy-start.14
  38.0 819.5 %all-gather.15.cloned.1.call-start = ((), (), s32[]{:S(2)}) async-start(), calls=%async_computation.3 | async-start | bytes 37748736 | tf_op jit(solution)/shard_map/all_gather | solution.py:29
  38.6 3.7 copy-start.5
  45.4 2.6 collective-permute-start.1
  48.1 966.0 %all-gather.11.cloned.1.call-start = ((), (), s32[]{:S(2)}) async-start(), calls=%async_computation.1 | async-start | bytes 37748736 | tf_op jit(solution)/shard_map/all_gather | solution.py:29
  48.2 3.6 copy-start.3
  55.0 2.9 copy-start.11
  55.0 3.0 copy-start.12
  55.0 2.8 collective-permute-start
  880.8 2.5 copy-start.16
  1171.1 0.7 copy-start.1
Sparse Core Ops, SparseCore 0:
  29.0 510.5 all-gather.12
  541.2 158.2 all-gather.8
  701.2 156.2 all-gather.14
  859.0 155.1 all-gather.10
where the time goes:
time: 1190 us; the launch traced here: 1180 us
  waiting for transfers between devices  744 us (63%)
  local copies, waits for them, and re-layouts  198 us (17%)
  matrix products  198 us (17%)
  other arithmetic  17.6 us (1%)
  between operations  14.5 us (1%)
    all_gather x2, waiting for transfers between devices, tile_update(): left_rows = lax.all_gather(left, 'col', axis=1)  614 us
    all_gather x2, waiting for transfers between devices, tile_update(): lax.all_gather(right_moved, 'row', axis=0)  130 us
    dot_general x8, matrix products, finish(): jnp.einsum('itkc,tujkc->iujc', left_blk, right_rows, preferred_element_ty...  127 us
    reshape x2, local copies, waits for them, and re-layouts, tile_update(): left_rows.reshape(block_count, block_rows, col_count, cols_loc, hidden)  55.8 us
    dynamic_slice x8, local copies, waits for them, and re-layouts, tile_update(): lax.map(finish, (left_rows.reshape(block_count, block_rows, col_count, co...  53.2 us
    while x4, local copies, waits for them, and re-layouts, tile_update(): lax.map(finish, (left_rows.reshape(block_count, block_rows, col_count, co...  46.8 us
    dot_general x16, matrix products, project(): jnp.einsum('ijd,de->ije', source, weight, preferred_element_type=jnp.floa...  40.4 us
    dot_general x8, matrix products, finish(): jnp.einsum('ijc,cd->ijd', normed_out, w_out, preferred_element_type=jnp.f...  30.5 us
  transfers between devices with their start and end apart: 6, of which 4 were waited for; matrix products, arithmetic and copies ran while one was open for 20% of the time, Pallas kernels for 0%

commit v1 on v0

v1 whole, which is shorter than its diff:
```python
import functools
import jax
import jax.numpy as jnp
from jax import lax
from jax.experimental import pallas as pl
from jax.experimental.pallas import tpu as pltpu
from jax.sharding import PartitionSpec as P

MESH = pl.DeviceIdType.MESH
F32 = jnp.float32
BF16 = jnp.bfloat16
EPS = 1e-5
STEPS = 2
ROWS = 16
VMEM_LIMIT = 60 * 1024 * 1024


def normalise_row(row, scale_col):
    values = row.astype(F32)
    count = values.shape[0]
    mean = jnp.sum(values, axis=0, keepdims=True) / count
    centered = values - mean
    variance = jnp.sum(centered * centered, axis=0, keepdims=True) / count
    return (centered * lax.rsqrt(variance + EPS) * scale_col).astype(BF16)


def project_kernel(z_ref, mask_ref, scale_ref, w_ref, a_ref, b_ref, sa, sb):
    rows, ch, cols = z_ref.shape
    hid = sa.shape[1]
    scale_col = scale_ref[...]

    def one_row(i, carry):
        normed = normalise_row(z_ref[i], scale_col)
        prod = jnp.dot(w_ref[...], normed, preferred_element_type=F32)
        mask = mask_ref[pl.ds(i, 1), :].astype(F32)
        sa[i] = mask * jax.nn.sigmoid(prod[:hid]) * prod[hid:2 * hid]
        sb[i] = mask * jax.nn.sigmoid(prod[2 * hid:3 * hid]) * prod[3 * hid:]
        return carry

    lax.fori_loop(0, rows, one_row, 0, unroll=2)
    for e in range(0, hid, 8):
        a_ref[e:e + 8] = jnp.transpose(sa[:, e:e + 8, :], (1, 0, 2)).astype(BF16)
        b_ref[0, e:e + 8] = jnp.transpose(sb[:, e:e + 8, :], (1, 0, 2)).astype(BF16)


def project(z_t, mask, scale_col, w_in):
    rows, ch, cols = z_t.shape
    hid = w_in.shape[0] // 4
    chunk = min(ROWS, rows // STEPS)
    per_step = rows // STEPS // chunk
    return pl.pallas_call(
        project_kernel,
        grid=(rows // chunk,),
        in_specs=[
            pl.BlockSpec((chunk, ch, cols), lambda i: (i, 0, 0)),
            pl.BlockSpec((chunk, cols), lambda i: (i, 0)),
            pl.BlockSpec((ch, 1), lambda i: (0, 0)),
            pl.BlockSpec((4 * hid, ch), lambda i: (0, 0)),
        ],
        out_specs=[
            pl.BlockSpec((hid, chunk, cols), lambda i: (0, i, 0)),
            pl.BlockSpec((1, hid, chunk, cols), lambda i: (i // per_step, 0, i % per_step, 0)),
        ],
        out_shape=[
            jax.ShapeDtypeStruct((hid, rows, cols), BF16),
            jax.ShapeDtypeStruct((STEPS, hid, rows // STEPS, cols), BF16),
        ],
        scratch_shapes=[pltpu.VMEM((chunk, hid, cols), F32), pltpu.VMEM((chunk, hid, cols), F32)],
        cost_estimate=pl.CostEstimate(flops=2 * rows * cols * ch * 4 * hid, bytes_accessed=rows * cols * ch * 6, transcendentals=rows * cols * hid * 2),
        name="project",
    )(z_t, mask, scale_col, w_in)


def finish_kernel(z_ref, n_ref, scale_ref, w_gate_ref, w_out_ref, o_ref, sn):
    rows, ch, cols = z_ref.shape
    steps, hid, _, lanes = n_ref.shape
    cores = cols // (lanes // 2 * steps) if steps > 1 else 1
    part = lanes // cores
    scale_col = scale_ref[...]
    for e in range(0, hid, 8):
        pieces = [jnp.transpose(n_ref[s, e:e + 8].astype(F32), (1, 0, 2)) for s in range(steps)]
        order = [pieces[s][:, :, r * part:(r + 1) * part] for r in range(cores) for s in range(steps)]
        sn[:, e:e + 8, :] = jnp.concatenate(order, axis=2)

    def one_row(i, carry):
        row = z_ref[i]
        normed = normalise_row(row, scale_col)
        gate = jax.nn.sigmoid(jnp.dot(w_gate_ref[...], normed, preferred_element_type=F32))
        update = jnp.dot(w_out_ref[...], sn[i].astype(BF16), preferred_element_type=F32)
        o_ref[i] = (row.astype(F32) + gate * update).astype(BF16)
        return carry

    lax.fori_loop(0, rows, one_row, 0, unroll=2)


def finish(z_t, n_all, which, scale_col, w_gate_t, w_out_t):
    rows, ch, cols = z_t.shape
    steps = STEPS
    hid, lanes = n_all.shape[1], n_all.shape[3]
    chunk = min(ROWS, rows)
    return pl.pallas_call(
        finish_kernel,
        grid=(rows // chunk,),
        in_specs=[
            pl.BlockSpec((chunk, ch, cols), lambda i: (i, 0, 0)),
            pl.BlockSpec((steps, hid, chunk, lanes), lambda i: (which, 0, i, 0)),
            pl.BlockSpec((ch, 1), lambda i: (0, 0)),
            pl.BlockSpec((ch, ch), lambda i: (0, 0)),
            pl.BlockSpec((ch, hid), lambda i: (0, 0)),
        ],
        out_specs=pl.BlockSpec((chunk, ch, cols), lambda i: (i, 0, 0)),
        out_shape=jax.ShapeDtypeStruct((rows, ch, cols), BF16),
        scratch_shapes=[pltpu.VMEM((chunk, hid, cols), F32)],
        cost_estimate=pl.CostEstimate(flops=4 * rows * cols * ch * hid, bytes_accessed=rows * cols * ch * 6, transcendentals=rows * cols * ch * 2),
        name="finish",
    )(z_t, n_all, scale_col, w_gate_t, w_out_t)


def exchange_kernel(ny, nx, cores, a0, a1, b0, b1, scale_ref,
                    n_out, a_all, a_relay, by, b_relay, bx, bo, n_relay,
                    a_v, b_v, o_v, ssum, st, st_in, mr, mr_in, nv, send_sems, recv_sems, loc_sems):
    a_in, b_in = (a0, a1), (b0, b1)
    crops = 2
    cb = o_v.shape[1]
    rows = o_v.shape[2]
    lanes = o_v.shape[3]
    sub = lanes // cores
    hid = cb * ny
    half = cb // 2
    y = lax.axis_index("col")
    row_id = lax.axis_index("row")
    x, r = row_id // cores, row_id % cores
    yy = [lax.rem(y + d, ny) for d in range(ny)]
    xr = [lax.rem(x + e, nx) * cores + r for e in range(nx)]
    partner = x * cores + (cores - 1 - r)
    to_y = [{"col": yy[d]} for d in range(ny)]
    to_x = [{"row": xr[e]} for e in range(nx)]
    to_p = {"row": partner}

    barrier = pltpu.get_barrier_semaphore()
    peers = to_y[1:] + [to_x[1], to_x[nx - 1], to_p]
    for dev in peers:
        pl.semaphore_signal(barrier, inc=1, device_id=dev, device_id_type=MESH)
    pl.semaphore_wait(barrier, len(peers))

    count = [0]
    sent = []

    def send(src, dst, dev):
        k = count[0]
        count[0] += 1
        copy = pltpu.make_async_remote_copy(
            src_ref=src, dst_ref=dst, send_sem=send_sems.at[k], recv_sem=recv_sems.at[k],
            device_id=dev, device_id_type=MESH)
        copy.start()
        sent.append(copy)
        return copy

    class AllToAll:
        def __init__(self, piece, direct, relay, onward):
            self.piece, self.direct, self.relay, self.onward = piece, direct, relay, onward

        def start(self):
            far = self.piece(2)
            self.r0 = send(far.at[:half], self.relay.at[0], to_y[1])
            self.r1 = send(far.at[half:], self.relay.at[1], to_y[3])
            self.c1 = send(self.piece(1), self.direct(1), to_y[1])
            self.c3 = send(self.piece(3), self.direct(3), to_y[3])

        def forward(self):
            self.r0.wait_recv()
            self.f0 = send(self.relay.at[0], self.onward(0).at[:half], to_y[1])
            self.r1.wait_recv()
            self.f1 = send(self.relay.at[1], self.onward(1).at[half:], to_y[3])

        def wait(self, d):
            if d == 1:
                self.c3.wait_recv()
            elif d == 3:
                self.c1.wait_recv()
            else:
                self.f0.wait_recv()
                self.f1.wait_recv()

    def a_unit(t):
        return AllToAll(lambda d: a_in[t].at[yy[d]], lambda d: a_all.at[t, 3 - d], a_relay.at[t], lambda h: a_all.at[t, 1])

    def b_unit(q):
        t, s = divmod(q, STEPS)
        return AllToAll(lambda d: b_in[t].at[s, yy[d]], lambda d: by.at[q, 3 - d], b_relay.at[q], lambda h: by.at[q, 1])

    def n_unit(q):
        return AllToAll(lambda d: nv.at[q, d], lambda d: n_out.at[q, y], n_relay.at[q],
                        lambda h: n_out.at[q, yy[3] if h == 0 else yy[1]])

    last = crops * STEPS
    ua = [a_unit(t) for t in range(crops)]
    ub = [b_unit(q) for q in range(last)]
    un = [n_unit(q) for q in range(last)]

    def own_piece(q, e, d):
        t, s = divmod(q, STEPS)
        if e == 0:
            return b_in[t].at[s, y] if d == 0 else by.at[q, d - 1]
        return bx.at[q, e - 1, d]

    xp, xm, xf, dd = {}, {}, {}, {}

    def x_direct(q, d):
        piece = own_piece(q, 0, d)
        xp[q, d] = send(piece, bx.at[q, 2, d], to_x[1])
        xm[q, d] = send(piece, bx.at[q, 0, d], to_x[3])

    def x_forward(q, d):
        xp[q, d].wait_recv()
        f0 = send(bx.at[q, 2, d].at[:half], bx.at[q, 1, d].at[:half], to_x[1])
        xm[q, d].wait_recv()
        f1 = send(bx.at[q, 0, d].at[half:], bx.at[q, 1, d].at[half:], to_x[3])
        xf[q, d] = (f0, f1)
        cross(q, 3, d)
        cross(q, 1, d)

    def x_far(q, d):
        for f in xf[q, d]:
            f.wait_recv()
        cross(q, 2, d)

    def cross(q, e, d):
        dd[q, e, d] = send(own_piece(q, e, d), bo.at[q, e, d], to_p)

    def local(src, dst, k):
        copy = pltpu.make_async_copy(src, dst, loc_sems.at[k])
        copy.start()
        return copy

    def load_b(q):
        copies = []
        for e in range(nx):
            for d in range(ny):
                dst = pl.ds(pl.multiple_of(e * lanes + r * sub, sub), sub)
                copies.append(local(own_piece(q, e, d), b_v.at[d, :, dst, :], len(copies)))
        for e in range(nx):
            for d in range(ny):
                dd[q, e, d].wait_recv()
                dst = pl.ds(pl.multiple_of(e * lanes + (cores - 1 - r) * sub, sub), sub)
                copies.append(local(bo.at[q, e, d], b_v.at[d, :, dst, :], len(copies)))
        return copies

    def load_a(t):
        base = 2 * nx * ny
        copies = [local(a_in[t].at[y], a_v.at[0], base)]
        for d in (1, 3, 2):
            ua[t].wait(d)
            copies.append(local(a_all.at[t, d - 1], a_v.at[d], base + d))
        return copies

    def contract(q):
        ssum[...] = jnp.zeros_like(ssum)

        def channel(c, carry):
            acc = None
            for d in range(ny):
                term = lax.dot_general(a_v[d, c], b_v[d, c], (((1,), (1,)), ((), ())), preferred_element_type=F32)
                acc = term if acc is None else acc + term
            for e in range(nx):
                part = acc[:, e * lanes:(e + 1) * lanes]
                o_v[e, c] = part
                ssum[e] += part
            return carry

        lax.fori_loop(0, cb, channel, 0)
        block = min(16, rows)

        def squares(k, carry):
            rs = pl.ds(pl.multiple_of(k * block, block), block)
            for e in range(nx):
                total = ssum[e, rs, :]
                mean = total * (1.0 / cb)
                acc = jnp.zeros_like(mean)
                for c in range(cb):
                    diff = o_v[e, c, rs, :] - mean
                    acc = acc + diff * diff
                st[q, e, 0, rs, :] = total
                st[q, e, 1, rs, :] = acc
            return carry

        lax.fori_loop(0, rows // block, squares, 0)

    e_of = [lax.rem(y + d + nx - x, nx) for d in range(ny)]
    stat, back = {}, {}

    def stats_send(q):
        for d in (2, 1, 3):
            stat[q, d] = send(st.at[q, e_of[d]], st_in.at[q, 3 - d], to_y[d])

    def stats_reduce(q):
        for d in (1, 3, 2):
            stat[q, d].wait_recv()
        mine = st[q, e_of[0]]
        parts = [mine] + [st_in[q, k] for k in range(ny - 1)]
        mean = (parts[0][0] + parts[1][0] + parts[2][0] + parts[3][0]) * (1.0 / hid)
        m2 = jnp.zeros_like(mean)
        for part in parts:
            diff = part[0] * (1.0 / cb) - mean
            m2 = m2 + part[1] + cb * (diff * diff)
        mr[q, 0] = mean
        mr[q, 1] = lax.rsqrt(m2 * (1.0 / hid) + EPS)

    def stats_back(q):
        for d in (2, 1, 3):
            back[q, d] = send(mr.at[q], mr_in.at[q, 3 - d], to_y[d])

    def apply_norm(q):
        for d in (0, 1, 3, 2):
            if d:
                back[q, 4 - d].wait_recv()
            mean = mr[q, 0] if d == 0 else mr_in[q, d - 1, 0]
            rstd = mr[q, 1] if d == 0 else mr_in[q, d - 1, 1]
            e = e_of[d]

            def channel(c, carry, mean=mean, rstd=rstd, e=e, d=d):
                nv[q, d, c] = ((o_v[e, c] - mean) * rstd * scale_ref[y * cb + c]).astype(BF16)
                return carry

            lax.fori_loop(0, cb, channel, 0)

    keep = []

    def n_send(q):
        keep.append(local(nv.at[q, 0], n_out.at[q, y], 2 * nx * ny + ny + q))
        un[q].start()

    ub[0].start()
    x_direct(0, 0)
    ua[0].start()
    ub[0].forward()
    for q in range(last + 1):
        t = q // STEPS
        if q < last:
            for d in (1, 3, 2):
                ub[q].wait(d)
                x_direct(q, d)
            for d in (0, 1, 3, 2):
                cross(q, 0, d)
        if q > 0:
            if (q - 1) % STEPS == 0:
                for copy in load_a((q - 1) // STEPS):
                    copy.wait()
            for copy in pending:
                copy.wait()
            contract(q - 1)
            stats_send(q - 1)
        if q + 1 < last:
            ub[q + 1].start()
            if (q + 1) % STEPS == 0:
                ua[(q + 1) // STEPS].start()
        if q < last and q % STEPS == 0:
            ua[t].forward()
        if q > 0:
            stats_reduce(q - 1)
            stats_back(q - 1)
        if q > 1:
            un[q - 2].forward()
        if q < last:
            x_forward(q, 0)
        if q > 0:
            apply_norm(q - 1)
            n_send(q - 1)
        if q < last:
            for d in (1, 3):
                x_forward(q, d)
            if q + 1 < last:
                ub[q + 1].forward()
                x_direct(q + 1, 0)
            x_forward(q, 2)
            for d in (0, 1, 3, 2):
                x_far(q, d)
            pending = load_b(q)
    un[last - 1].forward()
    for q in range(last):
        for d in (1, 3, 2):
            un[q].wait(d)
        keep[q].wait()
    for copy in sent:
        copy.wait_send()


def exchange(a_pair, b_pair, scale, ny, nx, cores):
    hid, rows, cols = a_pair[0].shape
    cb = hid // ny
    sub = rows // STEPS
    lanes = cores * sub
    q = 2 * STEPS
    a_pair = [a.reshape(ny, cb, rows, cols) for a in a_pair]
    b_pair = [b.reshape(STEPS, ny, cb, sub, cols) for b in b_pair]
    any_spec = pl.BlockSpec(memory_space=pl.ANY)

    def hbm(*shape):
        return jax.ShapeDtypeStruct(shape, BF16)

    sends = 2 * 6 + q * (6 + 4 * ny + nx * ny + 3 + 3 + 6)
    outs = pl.pallas_call(
        functools.partial(exchange_kernel, ny, nx, cores),
        in_specs=[any_spec] * 4 + [pl.BlockSpec(memory_space=pltpu.SMEM)],
        out_specs=[any_spec] * 8,
        out_shape=[
            hbm(q, ny, cb, rows, lanes),
            hbm(2, ny - 1, cb, rows, cols),
            hbm(2, 2, cb // 2, rows, cols),
            hbm(q, ny - 1, cb, sub, cols),
            hbm(q, 2, cb // 2, sub, cols),
            hbm(q, nx - 1, ny, cb, sub, cols),
            hbm(q, nx, ny, cb, sub, cols),
            hbm(q, 2, cb // 2, rows, lanes),
        ],
        scratch_shapes=[
            pltpu.VMEM((ny, cb, rows, cols), BF16),
            pltpu.VMEM((ny, cb, nx * lanes, cols), BF16),
            pltpu.VMEM((nx, cb, rows, lanes), F32),
            pltpu.VMEM((nx, rows, lanes), F32),
            pltpu.VMEM((q, nx, 2, rows, lanes), F32),
            pltpu.VMEM((q, ny - 1, 2, rows, lanes), F32),
            pltpu.VMEM((q, 2, rows, lanes), F32),
            pltpu.VMEM((q, ny - 1, 2, rows, lanes), F32),
            pltpu.VMEM((q, ny, cb, rows, lanes), BF16),
            pltpu.SemaphoreType.DMA((sends,)),
            pltpu.SemaphoreType.DMA((sends,)),
            pltpu.SemaphoreType.DMA((2 * nx * ny + ny + q,)),
        ],
        compiler_params=pltpu.CompilerParams(collective_id=0, has_side_effects=True, vmem_limit_bytes=VMEM_LIMIT),
        cost_estimate=pl.CostEstimate(flops=4 * rows * cols * hid * nx * cols, bytes_accessed=200000000, transcendentals=0),
        name="exchange",
    )(*a_pair, *b_pair, scale)
    return outs[0].reshape(q, hid, rows, lanes)


def solution(mesh):
    row_count = mesh.shape['row']
    col_count = mesh.shape['col']
    cores = row_count // col_count
    nx = row_count // cores
    pair_spec = P(('batch', 'row'), 'col', None)
    mask_spec = P(('batch', 'row'), 'col')
    replicated = P()

    def device_fn(z_one, z_two, mask_one, mask_two, ln_in_scale, w_a, w_a_gate, w_b, w_b_gate, w_gate, w_out, ln_out_scale):
        in_col = ln_in_scale.astype(F32)[:, None]
        w_in = jnp.concatenate([w_a_gate, w_a, w_b_gate, w_b], axis=1).T
        crops = [jnp.transpose(z, (0, 2, 1)) for z in (z_one, z_two)]
        ab = [project(z, m, in_col, w_in) for z, m in zip(crops, (mask_one, mask_two))]
        n_all = exchange([p[0] for p in ab], [p[1] for p in ab], ln_out_scale.astype(F32), col_count, nx, cores)
        outs = [finish(z, n_all, k, in_col, w_gate.T, w_out.T) for k, z in enumerate(crops)]
        return tuple(jnp.transpose(o, (0, 2, 1)) for o in outs)

    return jax.shard_map(
        device_fn,
        mesh=mesh,
        in_specs=(pair_spec, pair_spec, mask_spec, mask_spec) + (replicated,) * 8,
        out_specs=(pair_spec, pair_spec),
        check_vma=False,
    )
```

time: 1190 us -> 524 us (0.44)
  waiting for transfers between devices: 744 us -> 0 us
  Pallas kernels: 0 us -> 516 us
  matrix products: 198 us -> 0 us
  local copies, waits for them, and re-layouts: 198 us -> 5.32 us
  other arithmetic: 17.6 us -> 1.81 us
  between operations: 14.5 us -> 0.66 us
    all_gather x4 -> x0, waiting for transfers between devices: 744 us -> none  [the longest x2 614 us: tile_update(): left_rows = lax.all_gather(left, 'col', axis=1)]
    pallas_call x0 -> x5, Pallas kernels: none -> 516 us  [the longest x1 427 us: exchange(): pl.pallas_call(functools.partial(exchange_kernel, ny, nx, cores), in_spec...]
    dot_general x32 -> x0, matrix products: 198 us -> none  [the longest x8 127 us: finish(): jnp.einsum('itkc,tujkc->iujc', left_blk, right_rows, preferred_element_ty...]
    reshape x10 -> x0, local copies, waits for them, and re-layouts: 77.5 us -> none  [the longest x2 55.8 us: tile_update(): left_rows.reshape(block_count, block_rows, col_count, cols_loc, hidden)]
    dynamic_slice x8 -> x0, local copies, waits for them, and re-layouts: 53.2 us -> none  [tile_update(): lax.map(finish, (left_rows.reshape(block_count, block_rows, col_count, co...]
    while x4 -> x0, local copies, waits for them, and re-layouts: 46.8 us -> none  [tile_update(): lax.map(finish, (left_rows.reshape(block_count, block_rows, col_count, co...]
    transpose x8 -> x0, local copies, waits for them, and re-layouts: 13 us -> none  [finish(): jnp.einsum('itkc,tujkc->iujc', left_blk, right_rows, preferred_element_ty...]
  transfers between devices with their start and end apart: 6 -> 0, of which waited for: 4 -> 0; matrix products, arithmetic and copies ran while one was open for 20% -> 0% of each run, Pallas kernels for 0% -> 0%
where the time goes in v1:
time: 524 us
  Pallas kernels  516 us (98%)
  local copies, waits for them, and re-layouts  5.32 us (1%)
    pallas_call x1, Pallas kernels, exchange(): pl.pallas_call(functools.partial(exchange_kernel, ny, nx, cores), in_spec...  427 us
    pallas_call x2, Pallas kernels, project(): pl.pallas_call(project_kernel, grid=(rows // chunk,), in_specs=[pl.BlockS...  47.9 us
    pallas_call x2, Pallas kernels, finish(): pl.pallas_call(finish_kernel, grid=(rows // chunk,), in_specs=[pl.BlockSp...  40.3 us

profile of v1, /device:TPU:97, one launch (start us, length us, event | category | flops | bytes accessed | tf_op | source)
XLA Modules:
  0.0 523.5 jit_solution(4219176244506930414)
XLA Ops:
  0.6 0.7 bitcast_convert_fusion
  1.3 0.7 copy.18.scale_ref
  2.0 0.8 copy.14
  2.8 0.8 copy.15
  3.6 0.8 copy.16
  4.4 0.8 copy.17
  5.2 0.6 maximum_bitcast_fusion.w_ref
  5.9 23.9 %project.2 = (bf16[64,128,256]{2,1,0:T(8,128)(2,1)}, bf16[2,64,64,256]{3,2,1,0:T(8,128)(2,1)}) custom-call(bf16[128,64,256]{2,1,0:T(8,128)(2,1)} %bitcast.20, s32[128,256]{1,0:T(8,128)} %mask_ref.2, f32[64,1]{1,0:T(8,128)} %copy.18.scale_ref, bf16[256,64]{1,0:T(8,128)(2,1)} %maximum_bitcast_fusion.w_ref), custom_call_target="tpu_custom_call" | custom-call | flops 1073741824 | bytes 12582912 | tf_op jit(solution)/shard_map/project/pallas_call | solution.py:51
  29.8 0.0 copy-start.2
  29.8 24.0 %project.3 = (bf16[64,128,256]{2,1,0:T(8,128)(2,1)}, bf16[2,64,64,256]{3,2,1,0:T(8,128)(2,1)}) custom-call(bf16[128,64,256]{2,1,0:T(8,128)(2,1)} %bitcast.18, s32[128,256]{1,0:T(8,128)} %mask_ref.3, f32[64,1]{1,0:T(8,128)} %copy.18.scale_ref, bf16[256,64]{1,0:T(8,128)(2,1)} %maximum_bitcast_fusion.w_ref), custom_call_target="tpu_custom_call" | custom-call | flops 1073741824 | bytes 12582912 | tf_op jit(solution)/shard_map/project/pallas_call | solution.py:51
  53.7 0.0 copy-done.2
  53.7 0.5 convert_element_type.4.scale_ref
  54.3 0.0 copy-start
  54.3 0.0 copy-start.1
  54.3 427.5 %exchange.1 = (bf16[4,4,16,128,128]{4,3,2,1,0:T(8,128)(2,1)}, bf16[2,3,16,128,256]{4,3,2,1,0:T(8,128)(2,1)}, bf16[2,2,8,128,256]{4,3,2,1,0:T(8,128)(2,1)}, bf16[...) custom-call(bf16[4,16,128,256]{3,2,1,0:T(8,128)(2,1)} %bitcast.28, ...), custom_call_target="tpu_custom_call" | custom-call | flops 8589934592 | bytes 200000000 | tf_op jit(solution)/shard_map/exchange/pallas_call | solution.py:402
  481.8 0.0 copy-done
  481.8 0.7 copy.21
  482.5 0.0 copy-done.1
  482.5 0.7 copy.20
  483.2 20.2 %finish.3 = bf16[128,64,256]{2,1,0:T(8,128)(2,1)} custom-call(bf16[128,64,256]{2,1,0:T(8,128)(2,1)} %bitcast.19, bf16[4,64,128,128]{3,2,1,0:T(8,128)(2,1)} %bitcast.16, f32[64,1]{1,0:T(8,128)} %copy.18.scale_ref, bf16[64,64]{1,0:T(8,128)(2,1)} %bitcast.26, bf16[64,64]{1,0:T(8,128)(2,1)} %bitcast.24), custom_call_target="tpu_custom_call" | custom-call | flops 536870912 | bytes 12582912 | tf_op jit(solution)/shard_map/finish/pallas_call | solution.py:101
  503.3 20.2 %finish.2 = bf16[128,64,256]{2,1,0:T(8,128)(2,1)} custom-call(bf16[128,64,256]{2,1,0:T(8,128)(2,1)} %bitcast.21, bf16[4,64,128,128]{3,2,1,0:T(8,128)(2,1)} %bitcast.17, f32[64,1]{1,0:T(8,128)} %copy.18.scale_ref, bf16[64,64]{1,0:T(8,128)(2,1)} %bitcast.27, bf16[64,64]{1,0:T(8,128)(2,1)} %bitcast.25), custom_call_target="tpu_custom_call" | custom-call | flops 536870912 | bytes 12582912 | tf_op jit(solution)/shard_map/finish/pallas_call | solution.py:101
Async XLA Ops:
  29.8 24.0 %copy-start.2 = (bf16[64]{0:T(256)(128)(2,1)S(1)}, bf16[64]{0:T(256)(128)(2,1)}, u32[]{:S(2)}) copy-start(bf16[64]{0:T(256)(128)(2,1)} %param.23) | copy-start | bytes 388
  54.3 427.5 %copy-start = (bf16[64,64]{1,0:T(8,128)(2,1)S(1)}, bf16[64,64]{1,0:T(8,128)(2,1)}, u32[]{:S(2)}) copy-start(bf16[64,64]{1,0:T(8,128)(2,1)} %param.22) | copy-start | bytes 24580
  54.3 428.2 %copy-start.1 = (bf16[64,64]{1,0:T(8,128)(2,1)S(1)}, bf16[64,64]{1,0:T(8,128)(2,1)}, u32[]{:S(2)}) copy-start(bf16[64,64]{1,0:T(8,128)(2,1)} %param.21) | copy-start | bytes 24580
